TPU v7x, 32 devices: a 4x4x1 block of a 4x4x8 slice. The times are simulated.
32 devices in a mesh: dp: 1 (over z), inner: 4 (over y), vocab: 8 (over x, core).
Axes of the slice: x: 4, y: 4, z: 1, core: 2. Of those that a mesh axis runs over, the one named last changes fastest.
The devices are a block of a 4x4x8 slice.
Arguments:
- hidden: bfloat16 [256, 2304], P('dp')
- w_head: bfloat16 [2304, 256000], P(None, ('vocab', 'inner'))
- inv_temp: float32 [256], P('dp')
- target_id: int32 [256], P('dp')
Outputs:
- output 1: float32 [256, 256000], P('dp', ('vocab', 'inner'))
- output 2: float32 [256], P('dp')
All inputs are finite; a program needn't handle non-finite values.
Results may differ from a plain program's by a relative error of at most 0.001.
Values are sent between devices in bfloat16 or wider.
A program may use at most 768 MiB of HBM per device.

v0:
```python
import jax
import jax.numpy as jnp
from jax import lax
from jax.sharding import PartitionSpec as P

VOCAB_AXES = ('vocab', 'inner')


def solution(mesh):
    inner_count = mesh.shape['inner']

    def local_step(hidden, w_shard, inv_temp, target_id):
        width = w_shard.shape[1]
        logits = jnp.dot(hidden, w_shard, preferred_element_type=jnp.float32) * inv_temp[:, None]
        local_max = jnp.max(logits, axis=1)
        exp_local = jnp.exp(logits - local_max[:, None])
        local_sum = jnp.sum(exp_local, axis=1)
        global_max = lax.pmax(local_max, VOCAB_AXES)
        max_factor = jnp.exp(local_max - global_max)
        global_sum = lax.psum(local_sum * max_factor, VOCAB_AXES)
        row_scale = max_factor / global_sum
        local_cdf = jnp.cumsum(exp_local, axis=1) * row_scale[:, None]
        shard_total = local_cdf[:, -1]
        inner_idx = lax.axis_index('inner')
        vocab_idx = lax.axis_index('vocab')
        inner_totals = lax.all_gather(shard_total, 'inner')
        inner_mask = jnp.arange(inner_totals.shape[0]) < inner_idx
        inner_before = jnp.sum(jnp.where(inner_mask[:, None], inner_totals, 0.0), axis=0)
        chip_totals = lax.all_gather(jnp.sum(inner_totals, axis=0), 'vocab')
        chip_mask = jnp.arange(chip_totals.shape[0]) < vocab_idx
        chip_before = jnp.sum(jnp.where(chip_mask[:, None], chip_totals, 0.0), axis=0)
        cdf_table = local_cdf + (chip_before + inner_before)[:, None]
        shard_start = (vocab_idx * inner_count + inner_idx) * width
        local_col = target_id - shard_start
        picked = jnp.sum(jnp.where(jnp.arange(width)[None, :] == local_col[:, None], cdf_table, 0.0), axis=1)
        cdf_target = lax.psum(picked, VOCAB_AXES)
        return cdf_table, cdf_target

    return jax.shard_map(local_step, mesh=mesh, in_specs=(P('dp', None), P(None, VOCAB_AXES), P('dp'), P('dp')), out_specs=(P('dp', VOCAB_AXES), P('dp')), check_vma=False)
```

profile of v0, /device:TPU:97, one launch (start us, length us, event | category | flops | bytes accessed | tf_op | source)
XLA Modules:
  0.0 230.2 jit_solution(10429211319849626206)
XLA Ops:
  0.6 0.0 copy-start
  0.6 1.3 copy-done
  1.9 16.5 %fusion.6 = (f32[256]{0:T(256)S(1)}, f32[256,8000]{0,1:T(8,128)S(1)}) fusion(f32[256]{0:T(256)} %param.6, bf16[256,2304]{1,0:T(8,128)(2,1)S(1)} %copy-done, bf16[2304,8000]{0,1:T(8,128)(2,1)} %param.5), kind=kOutput, calls=%fused_computation.20 | convolution fusion | flops 9441280000 | bytes 46237696 | tf_op jit(solution)/shard_map/dot_general | solution.py:14
  18.4 4.4 %fusion.5 = (f32[256]{0:T(256)S(1)}, f32[256,8000]{0,1:T(8,128)}) fusion(f32[256,8000]{0,1:T(8,128)S(1)} %get-tuple-element.9, f32[256]{0:T(256)S(1)} %get-tuple-element.8), kind=kLoop, calls=%fused_computation.19 | loop fusion | flops 4095744 | bytes 16386048 | tf_op jit(solution)/shard_map/reduce_sum | solution.py:17
  22.8 49.7 %pmax.7 = f32[256]{0:T(256)S(1)} all-reduce(f32[256]{0:T(256)S(1)} %get-tuple-element.8), channel_id=1, replica_groups=mesh['dp'=1,'inner'=4,'vocab'=8] {'vocab','inner'}, use_global_device_ids=true, to_apply=%region_3.0 | all-reduce | flops 256 | bytes 2048 | tf_op jit(solution)/shard_map/pmax | solution.py:18
  72.5 43.3 %psum.14 = f32[256]{0:T(256)S(1)} all-reduce(f32[256]{0:T(256)S(1)} %fusion.4), channel_id=1, replica_groups=mesh['dp'=1,'inner'=4,'vocab'=8] {'vocab','inner'}, use_global_device_ids=true, to_apply=%region_5.6 | all-reduce | flops 256 | bytes 2048 | tf_op jit(solution)/shard_map/psum | solution.py:20
  115.9 7.0 %pad.3 = f32[256,8064]{0,1:T(8,128)} pad(f32[256,8000]{0,1:T(8,128)} %get-tuple-element.7, f32[]{:T(128)} %constant.7.clone.1), padding=0_0x0_64 | pad | bytes 16449540 | tf_op jit(solution)/shard_map/pad
  122.9 11.4 %fusion = f32[256,63,128]{0,1,2:T(8,128)} fusion(f32[256,63,128]{0,2,1:T(8,128)} %bitcast.15), kind=kOutput, calls=%fused_computation.1 | output fusion | flops 262176768 | bytes 16515072 | tf_op jit(solution)/shard_map/reduce-window
  134.3 0.8 slice_bitcast_fusion
  135.1 0.1 reduce-window.9
  135.2 4.2 %broadcast_add_fusion = f32[256,63,128]{0,1,2:T(8,128)S(1)} fusion(f32[256,63,128]{0,1,2:T(8,128)} %fusion, f32[256,63]{0,1:T(8,128)S(1)} %bitcast.16), kind=kLoop, calls=%fused_computation.7 | loop fusion | flops 2064384 | bytes 16579584 | tf_op jit(solution)/shard_map/reduce_window_sum
  139.4 4.8 %copy.10 = f32[256,63,128]{0,2,1:T(8,128)S(1)} copy(f32[256,63,128]{0,1,2:T(8,128)S(1)} %broadcast_add_fusion) | data formatting | bytes 16515072 | tf_op jit(solution)/shard_map/reduce_window_sum
  144.2 0.0 copy-start.2
  144.2 0.0 copy-start.3
  144.2 0.8 slice_multiply_fusion
  145.0 2.4 %copy-done.2 = f32[256,63,128]{0,2,1:T(8,128)} copy-done((f32[256,63,128]{0,2,1:T(8,128)}, f32[256,63,128]{0,2,1:T(8,128)S(1)}, u32[]{:S(2)}) %copy-start.2) | copy-done | bytes 8257560
  147.4 7.0 %all-gather = f32[1024,1]{0,1:T(1,128)S(1)} all-gather(f32[256,1]{0,1:T(1,128)S(1)} %slice.19), channel_id=2, replica_groups=mesh['dp'=1,'inner'=4,'vocab'=8] {'inner'}, dimensions={0}, use_global_device_ids=true | all-gather | bytes 5120 | tf_op jit(solution)/shard_map/all_gather | solution.py:26
  154.4 0.5 broadcast.23
  155.0 0.7 reduce.3
  155.6 0.1 select_reduce_fusion.1
  155.7 17.9 %all-gather.2 = f32[8,1,256]{2,1,0:T(1,128)S(1)} all-gather(f32[1,1,256]{2,1,0:T(1,128)S(1)} %bitcast.17), channel_id=3, replica_groups=mesh['dp'=1,'inner'=4,'vocab'=8] {'vocab'}, dimensions={0}, use_global_device_ids=true | all-gather | bytes 9216 | tf_op jit(solution)/shard_map/all_gather | solution.py:29
  173.6 0.1 fusion.2
  173.7 0.0 copy-done.3
  173.7 0.0 copy-start.1
  173.8 6.6 %select_reduce_fusion = (f32[256]{0:T(256)S(1)}, f32[256,8000]{0,1:T(8,128)}) fusion(s32[256]{0:T(256)S(1)} %broadcast_subtract_fusion, f32[256]{0:T(256)S(1)} %add.24, f32[256]{0:T(256)S(1)} %fusion.3, f32[256,8064]{0,1:T(8,128)} %bitcast.14), kind=kLoop, calls=%fused_computation.4 | loop fusion | flops 10239744 | bytes 16388096 | tf_op jit(solution)/shard_map/reduce_sum | solution.py:35
  180.3 49.8 %psum.15 = f32[256]{0:T(256)} all-reduce(f32[256]{0:T(256)S(1)} %get-tuple-element.4), channel_id=1, replica_groups=mesh['dp'=1,'inner'=4,'vocab'=8] {'vocab','inner'}, use_global_device_ids=true, to_apply=%region_10.11 | all-reduce | flops 256 | bytes 2048 | tf_op jit(solution)/shard_map/psum | solution.py:36
  230.2 0.0 copy-done.1
  (8 shorter events, 0.0 us)
Async XLA Ops:
  0.6 1.3 copy-start
  144.2 3.2 %copy-start.2 = (f32[256,63,128]{0,2,1:T(8,128)}, f32[256,63,128]{0,2,1:T(8,128)S(1)}, u32[]{:S(2)}) copy-start(f32[256,63,128]{0,2,1:T(8,128)S(1)} %copy.10) | copy-start | bytes 24772612
  144.2 29.5 %copy-start.3 = (s32[256]{0:T(256)S(1)}, s32[256]{0:T(256)}, u32[]{:S(2)}) copy-start(s32[256]{0:T(256)} %param.7) | copy-start | bytes 3076
  173.7 56.4 %copy-start.1 = (bf16[256,2304]{1,0:T(8,128)(2,1)S(1)}, bf16[256,2304]{1,0:T(8,128)(2,1)}, u32[]{:S(2)}) copy-start(bf16[256,2304]{1,0:T(8,128)(2,1)} %param.4) | copy-start | bytes 3538948
where the time goes:
time: 231 us; the launch traced here: 230 us
  blocking collectives  168 us (73%)
  other arithmetic  28.3 us (12%)
  local copies, waits for them, and re-layouts  16.8 us (7%)
  matrix products  16.5 us (7%)
    psum x1, blocking collectives, local_step(): cdf_target = lax.psum(picked, VOCAB_AXES)  49.8 us
    pmax x1, blocking collectives, local_step(): global_max = lax.pmax(local_max, VOCAB_AXES)  49.7 us
    psum x1, blocking collectives, local_step(): global_sum = lax.psum(local_sum * max_factor, VOCAB_AXES)  43.3 us
    all_gather x1, blocking collectives, local_step(): chip_totals = lax.all_gather(jnp.sum(inner_totals, axis=0), 'vocab')  17.9 us
    dot_general x1, matrix products, local_step(): jnp.dot(hidden, w_shard, preferred_element_type=jnp.float32)  16.5 us
    another operation x3, other arithmetic  15.7 us
    pad x1, local copies, waits for them, and re-layouts  7.05 us
    all_gather x1, blocking collectives, local_step(): inner_totals = lax.all_gather(shard_total, 'inner')  7.05 us

commit v1 on v0

v1 whole, which is shorter than its diff:
```python
import functools

import jax
import jax.numpy as jnp
from jax import lax
from jax.experimental import pallas as pl
from jax.experimental.pallas import tpu as pltpu
from jax.sharding import PartitionSpec as P

VOCAB_AXES = ('vocab', 'inner')
MESH = pl.DeviceIdType.MESH
LANES = 128
SUB = 8
TILE = 800


def stream_kernel(n_vocab, n_inner, h_hbm, w_hbm, inv_hbm, tgt_hbm,
                  c_ref, scale_ref, off_ref, ct_ref,
                  h_v, wbuf, inv_v, tgt_v, zbuf, z_top, m_tile, s_tile, t_tile,
                  stats, in_sem, w_sem, send_sem, recv_sem):
    peers = n_vocab * n_inner
    rows = h_v.shape[0]
    width = w_hbm.shape[0]
    halves = rows // LANES
    tiles = width // TILE
    run = TILE // SUB
    me = lax.axis_index('vocab') * n_inner + lax.axis_index('inner')

    def tokens(t):
        return pl.ds(pl.multiple_of(t * TILE, TILE), TILE)

    def w_copy(t):
        return pltpu.make_async_copy(w_hbm.at[tokens(t), :], wbuf.at[tokens(t), :], w_sem.at[t])

    small = [pltpu.make_async_copy(h_hbm, h_v, in_sem.at[0]),
             pltpu.make_async_copy(inv_hbm, inv_v, in_sem.at[1]),
             pltpu.make_async_copy(tgt_hbm, tgt_v, in_sem.at[2])]
    for copy in small:
        copy.start()

    @pl.loop(0, tiles)
    def _(t):
        w_copy(t).start()

    def peer(k):
        p = lax.rem(me + k, peers)
        return {'vocab': p // n_inner, 'inner': lax.rem(p, n_inner)}

    barrier = pltpu.get_barrier_semaphore()

    @pl.loop(1, peers)
    def _(k):
        pl.semaphore_signal(barrier, inc=1, device_id=peer(k), device_id_type=MESH)

    for copy in small:
        copy.wait()
    sub = lax.broadcasted_iota(jnp.int32, (SUB, LANES), 0)

    def logits(t):
        slot = lax.rem(t, 2)
        z = lax.dot_general(wbuf[tokens(t), :], h_v[...], (((1,), (1,)), ((), ())),
                            preferred_element_type=jnp.float32)
        for i in range(halves):
            zi = z[:, i * LANES:(i + 1) * LANES] * inv_v[pl.ds(i, 1), :]
            zbuf[slot, i] = zi
            z_top[slot, i] = jnp.max(zi.reshape(run, SUB, LANES), axis=0)

    def weigh(t):
        slot = lax.rem(t, 2)
        for i in range(halves):
            top = jnp.broadcast_to(jnp.max(z_top[slot, i], axis=0, keepdims=True), (SUB, LANES))
            goal = tgt_v[pl.ds(i, 1), :] - (me * width + t * TILE) - sub * run
            goal = jnp.minimum(goal, run - 1)
            total = jnp.zeros((SUB, LANES), jnp.float32)
            upto = jnp.zeros((SUB, LANES), jnp.float32)
            for j in range(run):
                total = total + jnp.exp(zbuf[slot, i, pl.ds(j, SUB, stride=run), :] - top)
                c_ref[i, pl.ds(pl.multiple_of(t * TILE + j * SUB, SUB), SUB), :] = total
                upto = jnp.where(goal == j, total, upto)
            m_tile[t, i] = top
            s_tile[t, i] = total
            t_tile[t, i] = upto

    w_copy(0).wait()
    logits(0)

    @pl.loop(1, tiles)
    def _(t):
        w_copy(t).wait()
        logits(t)
        weigh(t - 1)

    weigh(tiles - 1)

    mix = jnp.zeros((SUB, LANES), jnp.float32)
    for i in range(halves):
        m = m_tile[0, i]
        for t in range(1, tiles):
            m = jnp.maximum(m, m_tile[t, i])
        s = jnp.zeros((SUB, LANES), jnp.float32)
        u = jnp.zeros((SUB, LANES), jnp.float32)
        for t in range(tiles):
            f = jnp.exp(m_tile[t, i] - m)
            s = s + s_tile[t, i] * f
            u = u + t_tile[t, i] * f
        mix = jnp.where((sub == 4 * i) | (sub == 4 * i + 1), m, mix)
        mix = jnp.where(sub == 4 * i + 2, jnp.sum(s, axis=0, keepdims=True), mix)
        mix = jnp.where(sub == 4 * i + 3, jnp.sum(u, axis=0, keepdims=True), mix)
    stats[me] = mix

    pl.semaphore_wait(barrier, peers - 1)

    @pl.loop(1, peers)
    def _(k):
        pltpu.make_async_remote_copy(
            src_ref=stats.at[me], dst_ref=stats.at[me], send_sem=send_sem, recv_sem=recv_sem,
            device_id=peer(k), device_id_type=MESH).start()

    everyone = stats.at[pl.ds(0, peers - 1)]
    done = pltpu.make_async_remote_copy(
        src_ref=everyone, dst_ref=everyone, send_sem=send_sem, recv_sem=recv_sem,
        device_id=peer(0), device_id_type=MESH)
    done.wait_recv()

    peak = stats[0]
    for p in range(1, peers):
        peak = jnp.maximum(peak, stats[p])
    whole = jnp.zeros((SUB, LANES), jnp.float32)
    before = jnp.zeros((SUB, LANES), jnp.float32)
    for p in range(peers):
        part = pltpu.roll(jnp.exp(stats[p] - peak), 2, 0) * stats[p]
        whole = whole + part
        before = before + jnp.where(p < me, part, 0.0)
    offset = before / whole
    reached = whole / pltpu.roll(whole, 1, 0)
    for i in range(halves):
        def row(x, k):
            return jnp.broadcast_to(x[4 * i + k:4 * i + k + 1, :], (SUB, LANES))
        ct_ref[pl.ds(i, 1), :] = reached[4 * i + 3:4 * i + 4, :]
        m, s, base = row(peak, 0), row(whole, 2), row(offset, 2)
        for t in range(tiles):
            scale = jnp.exp(m_tile[t, i] - m) / s
            scale_ref[t, i] = scale
            mass = s_tile[t, i] * scale
            ahead = mass
            for d in (1, 2, 4):
                ahead = ahead + jnp.where(sub >= d, pltpu.roll(ahead, d, 0), 0.0)
            off_ref[t, i] = base + jnp.where(sub >= 1, pltpu.roll(ahead, 1, 0), 0.0)
            base = base + jnp.broadcast_to(ahead[SUB - 1:SUB, :], (SUB, LANES))
    done.wait_send()


def finish_kernel(c_ref, scale_ref, off_ref, ct_ref, out_hbm, ct_out, stage, sem):
    halves, width = c_ref.shape[:2]
    tiles = width // TILE
    run = TILE // SUB
    ct_out[...] = ct_ref[...]

    def copy(t, i):
        here = pl.ds(pl.multiple_of(t * TILE, TILE), TILE)
        return pltpu.make_async_copy(stage.at[i, here, :], out_hbm.at[here, pl.ds(i * LANES, LANES)], sem.at[i])

    @pl.loop(0, tiles)
    def _(t):
        for i in range(halves):
            scale, offset = scale_ref[t, i], off_ref[t, i]
            for j in range(run):
                v = c_ref[i, pl.ds(pl.multiple_of(t * TILE + j * SUB, SUB), SUB), :]
                stage[i, pl.ds(t * TILE + j, SUB, stride=run), :] = v * scale + offset
            copy(t, i).start()

    for i in range(halves):
        pltpu.make_async_copy(stage.at[i], out_hbm.at[:, pl.ds(i * LANES, LANES)], sem.at[i]).wait()


def solution(mesh):
    n_vocab, n_inner = mesh.shape['vocab'], mesh.shape['inner']
    peers = n_vocab * n_inner

    def local_step(hidden, w_shard, inv_temp, target_id):
        rows, depth = hidden.shape
        width = w_shard.shape[1]
        tiles = width // TILE
        halves = rows // LANES
        f32, bf16 = jnp.float32, jnp.bfloat16
        hbm = pl.BlockSpec(memory_space=pl.ANY)
        vmem = pl.BlockSpec(memory_space=pltpu.VMEM)
        c, scale, offset, ct = pl.pallas_call(
            functools.partial(stream_kernel, n_vocab, n_inner),
            out_shape=[pltpu.VMEM((halves, width, LANES), f32), pltpu.VMEM((tiles, halves, SUB, LANES), f32),
                       pltpu.VMEM((tiles, halves, SUB, LANES), f32), pltpu.VMEM((halves, LANES), f32)],
            in_specs=[hbm] * 4,
            out_specs=[vmem] * 4,
            scratch_shapes=[
                pltpu.VMEM((rows, depth), bf16),
                pltpu.VMEM((width, depth), bf16),
                pltpu.VMEM((halves, LANES), f32),
                pltpu.VMEM((halves, LANES), jnp.int32),
                pltpu.VMEM((2, halves, TILE, LANES), f32),
                pltpu.VMEM((2, halves, SUB, LANES), f32),
                pltpu.VMEM((tiles, halves, SUB, LANES), f32),
                pltpu.VMEM((tiles, halves, SUB, LANES), f32),
                pltpu.VMEM((tiles, halves, SUB, LANES), f32),
                pltpu.VMEM((peers, SUB, LANES), f32),
                pltpu.SemaphoreType.DMA((3,)),
                pltpu.SemaphoreType.DMA((tiles,)),
                pltpu.SemaphoreType.DMA,
                pltpu.SemaphoreType.DMA,
            ],
            compiler_params=pltpu.CompilerParams(
                collective_id=0, has_side_effects=True, vmem_limit_bytes=52 * 2**20),
        )(hidden, w_shard.T, inv_temp.reshape(halves, LANES), target_id.reshape(halves, LANES))
        table, target = pl.pallas_call(
            finish_kernel,
            out_shape=[pltpu.HBM((width, rows), f32), pltpu.HBM((halves, LANES), f32)],
            in_specs=[vmem] * 4,
            out_specs=[pl.BlockSpec(memory_space=pltpu.HBM), vmem],
            scratch_shapes=[pltpu.VMEM((halves, width, LANES), f32), pltpu.SemaphoreType.DMA((halves,))],
            compiler_params=pltpu.CompilerParams(vmem_limit_bytes=20 * 2**20),
        )(c, scale, offset, ct)
        return table.T, target.reshape(rows)

    return jax.shard_map(local_step, mesh=mesh, in_specs=(P('dp', None), P(None, VOCAB_AXES), P('dp'), P('dp')), out_specs=(P('dp', VOCAB_AXES), P('dp')), check_vma=False)
```

time: 231 us -> 31.1 us (0.13)
  blocking collectives: 168 us -> 0 us
  Pallas kernels: 0 us -> 30.4 us
  other arithmetic: 28.3 us -> 0 us
  local copies, waits for them, and re-layouts: 16.8 us -> 0 us
  matrix products: 16.5 us -> 0 us
    psum x2 -> x0, blocking collectives: 93.1 us -> none  [the longest x1 49.8 us: local_step(): cdf_target = lax.psum(picked, VOCAB_AXES)]
    pmax x1 -> x0, blocking collectives: 49.7 us -> none  [local_step(): global_max = lax.pmax(local_max, VOCAB_AXES)]
    pallas_call x0 -> x2, Pallas kernels: none -> 30.4 us  [the longest x1 26.6 us: local_step(): pl.pallas_call(functools.partial(stream_kernel, n_vocab, n_inner), out_sh...]
    all_gather x2 -> x0, blocking collectives: 24.9 us -> none  [the longest x1 17.9 us: local_step(): chip_totals = lax.all_gather(jnp.sum(inner_totals, axis=0), 'vocab')]
    dot_general x1 -> x0, matrix products: 16.5 us -> none  [local_step(): jnp.dot(hidden, w_shard, preferred_element_type=jnp.float32)]
    another operation x3 -> x0, other arithmetic: 15.7 us -> none
    reduce_sum x4 -> x0, other arithmetic: 11.2 us -> none  [the longest x1 6.58 us: local_step(): jnp.sum(jnp.where(jnp.arange(width)[None, :] == local_col[:, None], cdf_t...]
    pad x1 -> x0, local copies, waits for them, and re-layouts: 7.05 us -> none
where the time goes in v1:
time: 31.1 us
  Pallas kernels  30.4 us (98%)
  between operations  0.64 us (2%)
    pallas_call x1, Pallas kernels, local_step(): pl.pallas_call(functools.partial(stream_kernel, n_vocab, n_inner), out_sh...  26.6 us
    pallas_call x1, Pallas kernels, local_step(): pl.pallas_call(finish_kernel, out_shape=[pltpu.HBM((width, rows), f32), p...  3.83 us

profile of v1, /device:TPU:97, one launch (start us, length us, event | category | flops | bytes accessed | tf_op | source)
XLA Modules:
  0.0 31.1 jit_solution(8100712145546814414)
XLA Ops:
  0.6 26.6 %shard_map.59 = (f32[2,8000,128]{2,1,0:T(8,128)S(1)}, f32[10,2,8,128]{3,2,1,0:T(8,128)S(1)}, f32[10,2,8,128]{3,2,1,0:T(8,128)S(1)}, f32[2,128]{1,0:T(2,128)S(1)}) custom-call(bf16[256,2304]{1,0:T(8,128)(2,1)} %h_hbm.1, bf16[8000,2304]{1,0:T(8,128)(2,1)} %bitcast.5, f32[2,128]{1,0:T(2,128)} %bitcast.6, s32[2,128]{1,0:T(2,128)} %bitcast.7), custom_call_target="tpu_custom_call" | custom-call | tf_op jit(solution)/shard_map/pallas_call | solution.py:188
  27.2 3.8 %shard_map.60 = (f32[8000,256]{1,0:T(8,128)}, f32[2,128]{1,0:T(2,128)}) custom-call(f32[2,8000,128]{2,1,0:T(8,128)S(1)} %get-tuple-element.8.c_ref, f32[10,2,8,128]{3,2,1,0:T(8,128)S(1)} %get-tuple-element.9.scale_ref, f32[10,2,8,128]{3,2,1,0:T(8,128)S(1)} %get-tuple-element.10.off_ref, f32[2,128]{1,0:T(2,128)S(1)} %get-tuple-element.11.ct_ref), custom_call_target="tpu_custom_call" | custom-call | tf_op jit(solution)/shard_map/pallas_call | solution.py:213

commit v2 on v1

v2 whole, which is shorter than its diff:
```python
import functools

import jax
import jax.numpy as jnp
from jax import lax
from jax.experimental import pallas as pl
from jax.experimental.pallas import tpu as pltpu
from jax.sharding import PartitionSpec as P

VOCAB_AXES = ('vocab', 'inner')
MESH = pl.DeviceIdType.MESH
LANES = 128
SUB = 8
HEAD, BODY, TAIL = (320, 480), 800, (480, 320)


def plan(width):
    count = (width - sum(HEAD) - sum(TAIL)) // BODY
    sizes = list(HEAD) + [BODY] * count + list(TAIL)
    assert sum(sizes) == width
    starts = [sum(sizes[:i]) for i in range(len(sizes))]
    return list(zip(starts, sizes)), len(HEAD), count


def hint(x, k):
    return x if isinstance(x, int) else pl.multiple_of(x, k)


def above(x, sub):
    total = x
    for d in (1, 2, 4):
        total = total + jnp.where(sub >= d, pltpu.roll(total, d, 0), 0.0)
    return total - x, jnp.broadcast_to(total[SUB - 1:SUB, :], (SUB, LANES))


def stream_kernel(n_vocab, n_inner, h_hbm, w_hbm, inv_hbm, tgt_hbm,
                  c_ref, scale_ref, start_ref, ends_ref, ct_ref,
                  h_v, wbuf, inv_v, tgt_v, zbuf, ebuf, z_top, m_tile, s_tile, t_tile,
                  stats, in_sem, w_sem, send_sem, recv_sem):
    peers = n_vocab * n_inner
    rows = h_v.shape[0]
    width = w_hbm.shape[0]
    halves = rows // LANES
    tiles, heads, count = plan(width)
    my_vocab, my_inner = lax.axis_index('vocab'), lax.axis_index('inner')
    me = my_vocab * n_inner + my_inner
    sub = lax.broadcasted_iota(jnp.int32, (SUB, LANES), 0)

    def w_copy(t, start, size):
        here = pl.ds(hint(start, 16), size)
        return pltpu.make_async_copy(w_hbm.at[here, :], wbuf.at[here, :], w_sem.at[t])

    small = [pltpu.make_async_copy(h_hbm, h_v, in_sem.at[0]),
             pltpu.make_async_copy(inv_hbm, inv_v, in_sem.at[1]),
             pltpu.make_async_copy(tgt_hbm, tgt_v, in_sem.at[2])]
    for copy in small:
        copy.start()
    for t, (start, size) in enumerate(tiles):
        w_copy(t, start, size).start()

    far = sorted(((dv, di) for dv in range(n_vocab) for di in range(n_inner) if dv or di),
                 key=lambda o: -(min(o[0], n_vocab - o[0]) / 2 + min(o[1], n_inner - o[1])))

    def peer(dv, di):
        return {'vocab': lax.rem(my_vocab + dv, n_vocab), 'inner': lax.rem(my_inner + di, n_inner)}

    barrier = pltpu.get_barrier_semaphore()
    for offset in far:
        pl.semaphore_signal(barrier, inc=1, device_id=peer(*offset), device_id_type=MESH)

    for copy in small:
        copy.wait()

    def logits(start, size):
        z = lax.dot_general(wbuf[pl.ds(hint(start, 16), size), :], h_v[...], (((1,), (1,)), ((), ())),
                            preferred_element_type=jnp.float32)
        for i in range(halves):
            zi = z[:, i * LANES:(i + 1) * LANES] * inv_v[pl.ds(i, 1), :]
            zbuf[i, pl.ds(0, size), :] = zi
            z_top[i] = jnp.max(zi.reshape(size // SUB, SUB, LANES), axis=0)

    def weigh(t, start, size):
        run = size // SUB
        for i in range(halves):
            top = jnp.broadcast_to(jnp.max(z_top[i], axis=0, keepdims=True), (SUB, LANES))
            total = jnp.zeros((SUB, LANES), jnp.float32)
            for j in range(run):
                e = jnp.exp(zbuf[i, pl.ds(j, SUB, stride=run), :] - top)
                ebuf[i, pl.ds(j * SUB, SUB), :] = e
                total = total + e
            running, total = above(total, sub)
            goal = tgt_v[pl.ds(i, 1), :] - (me * width + start)
            upto = jnp.where((goal >= size) & (sub == 0), total, 0.0)
            goal = goal - sub * run
            for j in range(run):
                running = running + ebuf[i, pl.ds(j * SUB, SUB), :]
                c_ref[i, pl.ds(start + j, SUB, stride=run), :] = running
                upto = jnp.where(goal == j, running, upto)
            m_tile[t, i] = top
            s_tile[t, i] = total
            t_tile[t, i] = upto

    def step(t, start, size, before=None):
        w_copy(t, start, size).wait()
        if before is not None:
            weigh(t - 1, *before)
        logits(start, size)

    for t in range(heads + 1):
        step(t, *tiles[t], tiles[t - 1] if t else None)

    @pl.loop(heads + 1, heads + count)
    def _(t):
        start = tiles[heads][0] + (t - heads) * BODY
        step(t, start, BODY, (start - BODY, BODY))

    for t in range(heads + count, len(tiles)):
        step(t, *tiles[t], tiles[t - 1])
    weigh(len(tiles) - 1, *tiles[-1])

    mix = jnp.zeros((SUB, LANES), jnp.float32)
    for i in range(halves):
        m = m_tile[0, i]
        for t in range(1, len(tiles)):
            m = jnp.maximum(m, m_tile[t, i])
        s = jnp.zeros((SUB, LANES), jnp.float32)
        u = jnp.zeros((SUB, LANES), jnp.float32)
        for t in range(len(tiles)):
            f = jnp.exp(m_tile[t, i] - m)
            scale_ref[t, i] = f
            start_ref[t, i] = s
            s = s + s_tile[t, i] * f
            u = u + t_tile[t, i] * f
        mix = jnp.where((sub == 4 * i) | (sub == 4 * i + 1), m, mix)
        mix = jnp.where(sub == 4 * i + 2, s, mix)
        mix = jnp.where(sub == 4 * i + 3, jnp.sum(u, axis=0, keepdims=True), mix)
    stats[me] = mix

    pl.semaphore_wait(barrier, peers - 1)
    for offset in far:
        pltpu.make_async_remote_copy(
            src_ref=stats.at[me], dst_ref=stats.at[me], send_sem=send_sem, recv_sem=recv_sem,
            device_id=peer(*offset), device_id_type=MESH).start()

    everyone = stats.at[pl.ds(0, peers - 1)]
    done = pltpu.make_async_remote_copy(
        src_ref=everyone, dst_ref=everyone, send_sem=send_sem, recv_sem=recv_sem,
        device_id=peer(0, 0), device_id_type=MESH)
    done.wait_recv()

    peak = stats[0]
    for p in range(1, peers):
        peak = jnp.maximum(peak, stats[p])
    whole = jnp.zeros((SUB, LANES), jnp.float32)
    before = jnp.zeros((SUB, LANES), jnp.float32)
    for p in range(peers):
        part = pltpu.roll(jnp.exp(stats[p] - peak), 2, 0) * stats[p]
        whole = whole + part
        before = before + jnp.where(p < me, part, 0.0)
    factor = pltpu.roll(jnp.exp(stats[me] - peak), 2, 0) / whole
    offset = before / whole
    reached = whole / pltpu.roll(whole, 1, 0)
    for i in range(halves):
        ct_ref[pl.ds(i, 1), :] = reached[4 * i + 3:4 * i + 4, :]
        ends_ref[0, i] = jnp.broadcast_to(factor[4 * i + 2:4 * i + 3, :], (SUB, LANES))
        ends_ref[1, i] = jnp.broadcast_to(offset[4 * i + 2:4 * i + 3, :], (SUB, LANES))
    done.wait_send()


def finish_kernel(c_ref, scale_ref, start_ref, ends_ref, ct_ref, out_hbm, ct_out, stage, sem):
    halves, width = c_ref.shape[:2]
    tiles, heads, count = plan(width)
    ct_out[...] = ct_ref[...]

    def emit(t, start, size):
        first = start // SUB
        scale = [scale_ref[t, i] * ends_ref[0, i] for i in range(halves)]
        offset = [start_ref[t, i] * ends_ref[0, i] + ends_ref[1, i] for i in range(halves)]
        for k in range(size // SUB):
            for i in range(halves):
                v = c_ref[i, pl.ds(hint(start + k * SUB, SUB), SUB), :]
                stage[first + k, i] = v * scale[i] + offset[i]
        here = pl.ds(first, size // SUB)
        pltpu.make_async_copy(stage.at[here], out_hbm.at[here], sem).start()

    for t in range(heads):
        emit(t, *tiles[t])

    @pl.loop(heads, heads + count)
    def _(t):
        emit(t, tiles[heads][0] + (t - heads) * BODY, BODY)

    for t in range(heads + count, len(tiles)):
        emit(t, *tiles[t])

    pltpu.make_async_copy(stage, out_hbm, sem).wait()


def solution(mesh):
    n_vocab, n_inner = mesh.shape['vocab'], mesh.shape['inner']
    peers = n_vocab * n_inner
    f32, bf16 = jnp.float32, jnp.bfloat16
    hbm = pl.BlockSpec(memory_space=pl.ANY)
    vmem = pl.BlockSpec(memory_space=pltpu.VMEM)

    def local_step(hidden, w_shard, inv_temp, target_id):
        rows, depth = hidden.shape
        width = w_shard.shape[1]
        halves = rows // LANES
        tiles = len(plan(width)[0])
        small = (tiles, halves, SUB, LANES)
        packed = (width // SUB, halves, SUB, LANES)
        parts = pl.pallas_call(
            functools.partial(stream_kernel, n_vocab, n_inner),
            name='stream',
            out_shape=[pltpu.VMEM((halves, width, LANES), f32), pltpu.VMEM(small, f32), pltpu.VMEM(small, f32),
                       pltpu.VMEM((2, halves, SUB, LANES), f32), pltpu.VMEM((halves, LANES), f32)],
            in_specs=[hbm] * 4,
            out_specs=[vmem] * 5,
            scratch_shapes=[
                pltpu.VMEM((rows, depth), bf16),
                pltpu.VMEM((width, depth), bf16),
                pltpu.VMEM((halves, LANES), f32),
                pltpu.VMEM((halves, LANES), jnp.int32),
                pltpu.VMEM((halves, BODY, LANES), f32),
                pltpu.VMEM((halves, BODY, LANES), f32),
                pltpu.VMEM((halves, SUB, LANES), f32),
                pltpu.VMEM(small, f32),
                pltpu.VMEM(small, f32),
                pltpu.VMEM(small, f32),
                pltpu.VMEM((peers, SUB, LANES), f32),
                pltpu.SemaphoreType.DMA((3,)),
                pltpu.SemaphoreType.DMA((tiles,)),
                pltpu.SemaphoreType.DMA,
                pltpu.SemaphoreType.DMA,
            ],
            compiler_params=pltpu.CompilerParams(
                collective_id=0, has_side_effects=True, vmem_limit_bytes=52 * 2**20),
        )(hidden, w_shard.T, inv_temp.reshape(halves, LANES), target_id.reshape(halves, LANES))
        table, target = pl.pallas_call(
            finish_kernel,
            name='finish',
            out_shape=[pltpu.HBM(packed, f32), pltpu.HBM((halves, LANES), f32)],
            in_specs=[vmem] * 5,
            out_specs=[pl.BlockSpec(memory_space=pltpu.HBM), vmem],
            scratch_shapes=[pltpu.VMEM(packed, f32), pltpu.SemaphoreType.DMA],
            compiler_params=pltpu.CompilerParams(vmem_limit_bytes=20 * 2**20),
        )(*parts)
        return table.transpose(0, 2, 1, 3).reshape(width, rows).T, target.reshape(rows)

    return jax.shard_map(local_step, mesh=mesh, in_specs=(P('dp', None), P(None, VOCAB_AXES), P('dp'), P('dp')), out_specs=(P('dp', VOCAB_AXES), P('dp')), check_vma=False)
```

time: 31.1 us -> 40.8 us (1.31)
  Pallas kernels: 30.4 us -> 40.1 us
    pallas_call x2, Pallas kernels: 30.4 us -> 40.1 us  [the longest x1 36.3 us: local_step(): pl.pallas_call(functools.partial(stream_kernel, n_vocab, n_inner), name='...]
where the time goes in v2:
time: 40.8 us
  Pallas kernels  40.1 us (98%)
  between operations  0.64 us (2%)
    pallas_call x1, Pallas kernels, local_step(): pl.pallas_call(functools.partial(stream_kernel, n_vocab, n_inner), name='...  36.3 us
    pallas_call x1, Pallas kernels, local_step(): pl.pallas_call(finish_kernel, name='finish', out_shape=[pltpu.HBM(packed,...  3.83 us

profile of v2, /device:TPU:97, one launch (start us, length us, event | category | flops | bytes accessed | tf_op | source)
XLA Modules:
  0.0 40.8 jit_solution(9635358203060184986)
XLA Ops:
  0.6 36.3 %stream.1 = (f32[2,8000,128]{2,1,0:T(8,128)S(1)}, f32[12,2,8,128]{3,2,1,0:T(8,128)S(1)}, f32[12,2,8,128]{3,2,1,0:T(8,128)S(1)}, f32[2,2,8,128]{3,2,1,0:T(8,128)S(1)}, f32[2,128]{1,0:T(2,128)S(1)}) custom-call(bf16[256,2304]{1,0:T(8,128)(2,1)} %h_hbm.1, bf16[8000,2304]{1,0:T(8,128)(2,1)} %bitcast.9, f32[2,128]{1,0:T(2,128)} %bitcast.10, s32[2,128]{1,0:T(2,128)} %bitcast.11), custom_call_target="tpu_custom_call" | custom-call | tf_op jit(solution)/shard_map/stream/pallas_call | solution.py:213
  36.9 3.8 %finish.1 = (f32[1000,2,8,128]{3,2,1,0:T(8,128)}, f32[2,128]{1,0:T(2,128)}) custom-call(f32[2,8000,128]{2,1,0:T(8,128)S(1)} %get-tuple-element.9.c_ref, f32[12,2,8,128]{3,2,1,0:T(8,128)S(1)} %get-tuple-element.10.scale_ref, f32[12,2,8,128]{3,2,1,0:T(8,128)S(1)} %get-tuple-element.11.start_ref, f32[2,2,8,128]{3,2,1,0:T(8,128)S(1)} %get-tuple-element.12.ends_ref, ...), custom_call_target="tpu_custom_call" | custom-call | tf_op jit(solution)/shard_map/finish/pallas_call | solution.py:240

commit v3 on v2

v3 whole, which is shorter than its diff:
```python
import functools

import jax
import jax.numpy as jnp
from jax import lax
from jax.experimental import pallas as pl
from jax.experimental.pallas import tpu as pltpu
from jax.sharding import PartitionSpec as P

VOCAB_AXES = ('vocab', 'inner')
MESH = pl.DeviceIdType.MESH
LANES = 128
SUB = 8
BODY = 800
WIDE = 256
BLOCKS = 25


def hint(x, k):
    return x if isinstance(x, int) else pl.multiple_of(x, k)


def above(x, sub):
    total = x
    for d in (1, 2, 4):
        total = total + jnp.where(sub >= d, pltpu.roll(total, d, 0), 0.0)
    return total - x, jnp.broadcast_to(total[SUB - 1:SUB, :], (SUB, LANES))


def stream_kernel(h_hbm, w_hbm, inv_hbm, tgt_hbm,
                  c_ref, scale_ref, start_ref, mix_ref,
                  h_v, wbuf, inv_v, tgt_v, zbuf, ebuf, m_tile, s_tile, t_tile, in_sem, w_sem):
    rows, depth = h_v.shape
    width = w_hbm.shape[0]
    halves = rows // LANES
    count = width // BODY
    part = BODY // 2
    run = BODY // SUB
    me = lax.axis_index('vocab') * lax.axis_size('inner') + lax.axis_index('inner')
    sub = lax.broadcasted_iota(jnp.int32, (SUB, LANES), 0)

    def w_copy(t):
        here = pl.ds(hint(t * BODY, 16), BODY)
        return pltpu.make_async_copy(w_hbm.at[here, :], wbuf.at[here, :], w_sem.at[t])

    small = [pltpu.make_async_copy(h_hbm, h_v, in_sem.at[0]),
             pltpu.make_async_copy(inv_hbm, inv_v, in_sem.at[1]),
             pltpu.make_async_copy(tgt_hbm, tgt_v, in_sem.at[2])]
    for copy in small:
        copy.start()

    @pl.loop(0, count)
    def _(t):
        w_copy(t).start()

    for copy in small:
        copy.wait()

    def weigh(t, tops):
        start = t * BODY
        for i in range(halves):
            top = jnp.broadcast_to(jnp.max(tops[i], axis=0, keepdims=True), (SUB, LANES))
            sums = [jnp.zeros((SUB, LANES), jnp.float32)] * 4
            for j in range(run):
                e = jnp.exp(zbuf[i, pl.ds(j, SUB, stride=run), :] - top)
                ebuf[i, pl.ds(j * SUB, SUB), :] = e
                sums[j % 4] = sums[j % 4] + e
            running, total = above((sums[0] + sums[1]) + (sums[2] + sums[3]), sub)
            goal = tgt_v[pl.ds(i, 1), :] - (me * width + start)
            upto = jnp.where((goal >= BODY) & (sub == 0), total, 0.0)
            goal = goal - sub * run
            for j in range(run):
                running = running + ebuf[i, pl.ds(j * SUB, SUB), :]
                c_ref[i, pl.ds(start + j, SUB, stride=run), :] = running
                upto = jnp.where(goal == j, running, upto)
            m_tile[t, i] = top
            s_tile[t, i] = total
            t_tile[t, i] = upto

    def multiply(*accs):
        accs = (accs[:2], accs[2:])

        def push(k):
            for q in range(2):
                pltpu.matmul_push_rhs(h_v[:, pl.ds(k * WIDE, WIDE)], 0, q, transpose=True)

        def drain(t, slot):
            tops = [None] * halves
            for q in range(2):
                z = pltpu.matmul_pop(accs[q][slot])
                for i in range(halves):
                    zi = z[:, i * LANES:(i + 1) * LANES] * inv_v[pl.ds(i, 1), :]
                    zbuf[i, pl.ds(q * part, part), :] = zi
                    top = jnp.max(zi.reshape(part // SUB, SUB, LANES), axis=0)
                    tops[i] = top if q == 0 else jnp.maximum(tops[i], top)
            weigh(t, tops)

        def step(t, slot, first=False, final=False):
            w_copy(t).wait()
            for k in range(depth // WIDE):
                for q in range(2):
                    pltpu.matmul_acc_lhs(
                        accs[q][slot], wbuf[pl.ds(hint(t * BODY + q * part, 16), part), pl.ds(k * WIDE, WIDE)],
                        load_staged_rhs=0)
                if k < depth // WIDE - 1:
                    push(k + 1)
                elif not final:
                    push(0)
                if k == 1 and not first:
                    drain(t - 1, 1 - slot)

        for q in range(2):
            for slot in range(2):
                pltpu.matmul_pop(accs[q][slot])
        push(0)
        step(0, 0, first=True)
        step(1, 1)

        @pl.loop(1, count // 2 - 1)
        def _(p):
            step(2 * p, 0)
            step(2 * p + 1, 1)

        step(count - 2, 0)
        step(count - 1, 1, final=True)
        drain(count - 1, 1)

    pl.run_scoped(multiply, *[pltpu.ACC(q)((part, rows), jnp.float32) for q in (0, 0, 1, 1)])

    mix = jnp.zeros((SUB, LANES), jnp.float32)
    for i in range(halves):
        m = m_tile[0, i]
        for t in range(1, count):
            m = jnp.maximum(m, m_tile[t, i])
        s = jnp.zeros((SUB, LANES), jnp.float32)
        u = jnp.zeros((SUB, LANES), jnp.float32)
        for t in range(count):
            f = jnp.exp(m_tile[t, i] - m)
            scale_ref[t, i] = f
            start_ref[t, i] = s
            s = s + s_tile[t, i] * f
            u = u + t_tile[t, i] * f
        mix = jnp.where((sub == 4 * i) | (sub == 4 * i + 1), m, mix)
        mix = jnp.where(sub == 4 * i + 2, s, mix)
        mix = jnp.where(sub == 4 * i + 3, jnp.sum(u, axis=0, keepdims=True), mix)
    mix_ref[...] = mix


def exchange_kernel(n_vocab, n_inner, mix_ref, ends_ref, ct_ref, stats, send_sem, recv_sem):
    peers = n_vocab * n_inner
    halves = ct_ref.shape[0]
    my_vocab, my_inner = lax.axis_index('vocab'), lax.axis_index('inner')
    me = my_vocab * n_inner + my_inner

    far = sorted(((dv, di) for dv in range(n_vocab) for di in range(n_inner) if dv or di),
                 key=lambda o: -(min(o[0], n_vocab - o[0]) / 2 + min(o[1], n_inner - o[1])))

    def peer(dv, di):
        return {'vocab': lax.rem(my_vocab + dv, n_vocab), 'inner': lax.rem(my_inner + di, n_inner)}

    stats[me] = mix_ref[...]
    barrier = pltpu.get_barrier_semaphore()
    for offset in far:
        pl.semaphore_signal(barrier, inc=1, device_id=peer(*offset), device_id_type=MESH)
    pl.semaphore_wait(barrier, peers - 1)
    for offset in far:
        pltpu.make_async_remote_copy(
            src_ref=stats.at[me], dst_ref=stats.at[me], send_sem=send_sem, recv_sem=recv_sem,
            device_id=peer(*offset), device_id_type=MESH).start()

    everyone = stats.at[pl.ds(0, peers - 1)]
    done = pltpu.make_async_remote_copy(
        src_ref=everyone, dst_ref=everyone, send_sem=send_sem, recv_sem=recv_sem,
        device_id=peer(0, 0), device_id_type=MESH)
    done.wait_recv()

    peak = stats[0]
    for p in range(1, peers):
        peak = jnp.maximum(peak, stats[p])
    whole = jnp.zeros((SUB, LANES), jnp.float32)
    before = jnp.zeros((SUB, LANES), jnp.float32)
    for p in range(peers):
        mass = pltpu.roll(jnp.exp(stats[p] - peak), 2, 0) * stats[p]
        whole = whole + mass
        before = before + jnp.where(p < me, mass, 0.0)
    factor = pltpu.roll(jnp.exp(stats[me] - peak), 2, 0) / whole
    offset = before / whole
    reached = whole / pltpu.roll(whole, 1, 0)
    for i in range(halves):
        ct_ref[pl.ds(i, 1), :] = reached[4 * i + 3:4 * i + 4, :]
        ends_ref[0, i] = jnp.broadcast_to(factor[4 * i + 2:4 * i + 3, :], (SUB, LANES))
        ends_ref[1, i] = jnp.broadcast_to(offset[4 * i + 2:4 * i + 3, :], (SUB, LANES))
    done.wait_send()


def finish_kernel(c_ref, scale_ref, start_ref, ends_ref, ct_ref, out_hbm, ct_out, stage, sem):
    halves, width = c_ref.shape[:2]
    parts = BODY // SUB // BLOCKS
    ct_out[...] = ct_ref[...]

    @pl.loop(0, width // SUB // BLOCKS)
    def _(b):
        t = b // parts
        scale = [scale_ref[t, i] * ends_ref[0, i] for i in range(halves)]
        offset = [start_ref[t, i] * ends_ref[0, i] + ends_ref[1, i] for i in range(halves)]
        first = b * BLOCKS
        for k in range(BLOCKS):
            for i in range(halves):
                v = c_ref[i, pl.ds(hint((first + k) * SUB, SUB), SUB), :]
                stage[first + k, i] = v * scale[i] + offset[i]
        here = pl.ds(first, BLOCKS)
        pltpu.make_async_copy(stage.at[here], out_hbm.at[here], sem).start()

    pltpu.make_async_copy(stage, out_hbm, sem).wait()


def solution(mesh):
    n_vocab, n_inner = mesh.shape['vocab'], mesh.shape['inner']
    peers = n_vocab * n_inner
    f32, bf16 = jnp.float32, jnp.bfloat16
    hbm = pl.BlockSpec(memory_space=pl.ANY)
    vmem = pl.BlockSpec(memory_space=pltpu.VMEM)

    def local_step(hidden, w_shard, inv_temp, target_id):
        rows, depth = hidden.shape
        width = w_shard.shape[1]
        halves = rows // LANES
        tiles = width // BODY
        small = (tiles, halves, SUB, LANES)
        packed = (width // SUB, halves, SUB, LANES)
        c, scale, start, mix = pl.pallas_call(
            stream_kernel,
            name='stream',
            out_shape=[pltpu.VMEM((halves, width, LANES), f32), pltpu.VMEM(small, f32), pltpu.VMEM(small, f32),
                       pltpu.VMEM((SUB, LANES), f32)],
            in_specs=[hbm] * 4,
            out_specs=[vmem] * 4,
            scratch_shapes=[
                pltpu.VMEM((rows, depth), bf16),
                pltpu.VMEM((width, depth), bf16),
                pltpu.VMEM((halves, LANES), f32),
                pltpu.VMEM((halves, LANES), jnp.int32),
                pltpu.VMEM((halves, BODY, LANES), f32),
                pltpu.VMEM((halves, BODY, LANES), f32),
                pltpu.VMEM(small, f32),
                pltpu.VMEM(small, f32),
                pltpu.VMEM(small, f32),
                pltpu.SemaphoreType.DMA((3,)),
                pltpu.SemaphoreType.DMA((tiles,)),
            ],
            compiler_params=pltpu.CompilerParams(vmem_limit_bytes=52 * 2**20),
        )(hidden, w_shard.T, inv_temp.reshape(halves, LANES), target_id.reshape(halves, LANES))
        ends, ct = pl.pallas_call(
            functools.partial(exchange_kernel, n_vocab, n_inner),
            name='exchange',
            out_shape=[pltpu.VMEM((2, halves, SUB, LANES), f32), pltpu.VMEM((halves, LANES), f32)],
            in_specs=[vmem],
            out_specs=[vmem] * 2,
            scratch_shapes=[pltpu.VMEM((peers, SUB, LANES), f32), pltpu.SemaphoreType.DMA, pltpu.SemaphoreType.DMA],
            compiler_params=pltpu.CompilerParams(collective_id=0, has_side_effects=True, vmem_limit_bytes=2**20),
        )(mix)
        table, target = pl.pallas_call(
            finish_kernel,
            name='finish',
            out_shape=[pltpu.HBM(packed, f32), pltpu.HBM((halves, LANES), f32)],
            in_specs=[vmem] * 5,
            out_specs=[pl.BlockSpec(memory_space=pltpu.HBM), vmem],
            scratch_shapes=[pltpu.VMEM(packed, f32), pltpu.SemaphoreType.DMA],
            compiler_params=pltpu.CompilerParams(vmem_limit_bytes=20 * 2**20),
        )(c, scale, start, ends, ct)
        return table.transpose(0, 2, 1, 3).reshape(width, rows).T, target.reshape(rows)

    return jax.shard_map(local_step, mesh=mesh, in_specs=(P('dp', None), P(None, VOCAB_AXES), P('dp'), P('dp')), out_specs=(P('dp', VOCAB_AXES), P('dp')), check_vma=False)
```

time: 40.8 us -> 30.8 us (0.75)
  Pallas kernels: 40.1 us -> 30 us
    pallas_call x1 -> x2, Pallas kernels: 36.3 us -> 26.2 us  [the longest x1 13.5 us: local_step(): pl.pallas_call(stream_kernel, name='stream', out_shape=[pltpu.VMEM((halve...]
where the time goes in v3:
time: 30.8 us; the launch traced here: 30.7 us
  Pallas kernels  30 us (97%)
  between operations  0.65 us (2%)
    pallas_call x1, Pallas kernels, local_step(): pl.pallas_call(stream_kernel, name='stream', out_shape=[pltpu.VMEM((halve...  13.5 us
    pallas_call x1, Pallas kernels, local_step(): pl.pallas_call(functools.partial(exchange_kernel, n_vocab, n_inner), name...  12.8 us
    pallas_call x1, Pallas kernels, local_step(): pl.pallas_call(finish_kernel, name='finish', out_shape=[pltpu.HBM(packed,...  3.8 us

profile of v3, /device:TPU:97, one launch (start us, length us, event | category | flops | bytes accessed | tf_op | source)
XLA Modules:
  0.0 30.7 jit_solution(11796809763764555794)
XLA Ops:
  0.6 13.5 %stream.1 = (f32[2,8000,128]{2,1,0:T(8,128)S(1)}, f32[10,2,8,128]{3,2,1,0:T(8,128)S(1)}, f32[10,2,8,128]{3,2,1,0:T(8,128)S(1)}, f32[8,128]{1,0:T(8,128)S(1)}) custom-call(bf16[256,2304]{1,0:T(8,128)(2,1)} %h_hbm.1, bf16[8000,2304]{1,0:T(8,128)(2,1)} %bitcast.9, f32[2,128]{1,0:T(2,128)} %bitcast.10, s32[2,128]{1,0:T(2,128)} %bitcast.11), custom_call_target="tpu_custom_call" | custom-call | tf_op jit(solution)/shard_map/stream/pallas_call | solution.py:231
  14.1 12.8 %exchange.1 = (f32[2,2,8,128]{3,2,1,0:T(8,128)S(1)}, f32[2,128]{1,0:T(2,128)S(1)}) custom-call(f32[8,128]{1,0:T(8,128)S(1)} %get-tuple-element.13.mix_ref), custom_call_target="tpu_custom_call" | custom-call | tf_op jit(solution)/shard_map/exchange/pallas_call | solution.py:253
  26.9 3.8 %finish.1 = (f32[1000,2,8,128]{3,2,1,0:T(8,128)}, f32[2,128]{1,0:T(2,128)}) custom-call(f32[2,8000,128]{2,1,0:T(8,128)S(1)} %get-tuple-element.10.c_ref, f32[10,2,8,128]{3,2,1,0:T(8,128)S(1)} %get-tuple-element.11.scale_ref, f32[10,2,8,128]{3,2,1,0:T(8,128)S(1)} %get-tuple-element.12.start_ref, f32[2,2,8,128]{3,2,1,0:T(8,128)S(1)} %get-tuple-element.14.ends_ref, ...), custom_call_target="tpu_custom_call" | custom-call | tf_op jit(solution)/shard_map/finish/pallas_call | solution.py:262

commit v4 on v3

--- a/solution.py
+++ b/solution.py
@@ -196,7 +196,8 @@
 def finish_kernel(c_ref, scale_ref, start_ref, ends_ref, ct_ref, out_hbm, ct_out, stage, sem):
     halves, width = c_ref.shape[:2]
     parts = BODY // SUB // BLOCKS
-    ct_out[...] = ct_ref[...]
+    target = pltpu.make_async_copy(ct_ref, ct_out, sem.at[1])
+    target.start()
 
     @pl.loop(0, width // SUB // BLOCKS)
     def _(b):
@@ -209,9 +210,10 @@
                 v = c_ref[i, pl.ds(hint((first + k) * SUB, SUB), SUB), :]
                 stage[first + k, i] = v * scale[i] + offset[i]
         here = pl.ds(first, BLOCKS)
-        pltpu.make_async_copy(stage.at[here], out_hbm.at[here], sem).start()
-
-    pltpu.make_async_copy(stage, out_hbm, sem).wait()
+        pltpu.make_async_copy(stage.at[here], out_hbm.at[here], sem.at[0]).start()
+
+    pltpu.make_async_copy(stage, out_hbm, sem.at[0]).wait()
+    target.wait()
 
 
 def solution(mesh):
@@ -264,8 +266,8 @@
             name='finish',
             out_shape=[pltpu.HBM(packed, f32), pltpu.HBM((halves, LANES), f32)],
             in_specs=[vmem] * 5,
-            out_specs=[pl.BlockSpec(memory_space=pltpu.HBM), vmem],
-            scratch_shapes=[pltpu.VMEM(packed, f32), pltpu.SemaphoreType.DMA],
+            out_specs=[pl.BlockSpec(memory_space=pltpu.HBM)] * 2,
+            scratch_shapes=[pltpu.VMEM(packed, f32), pltpu.SemaphoreType.DMA((2,))],
             compiler_params=pltpu.CompilerParams(vmem_limit_bytes=20 * 2**20),
         )(c, scale, start, ends, ct)
         return table.transpose(0, 2, 1, 3).reshape(width, rows).T, target.reshape(rows)

time: 30.8 us -> 30.2 us (0.981)
  Pallas kernels: 30 us -> 29.5 us
    pallas_call x1, Pallas kernels: 3.8 us -> 3.25 us  [local_step(): pl.pallas_call(finish_kernel, name='finish', out_shape=[pltpu.HBM(packed,...]
where the time goes in v4:
time: 30.2 us; the launch traced here: 30.1 us
  Pallas kernels  29.5 us (98%)
  between operations  0.65 us (2%)
    pallas_call x1, Pallas kernels, local_step(): pl.pallas_call(stream_kernel, name='stream', out_shape=[pltpu.VMEM((halve...  13.5 us
    pallas_call x1, Pallas kernels, local_step(): pl.pallas_call(functools.partial(exchange_kernel, n_vocab, n_inner), name...  12.8 us
    pallas_call x1, Pallas kernels, local_step(): pl.pallas_call(finish_kernel, name='finish', out_shape=[pltpu.HBM(packed,...  3.25 us

profile of v4, /device:TPU:97, one launch (start us, length us, event | category | flops | bytes accessed | tf_op | source)
XLA Modules:
  0.0 30.1 jit_solution(4878818857021248100)
XLA Ops:
  0.6 13.5 %stream.1 = (f32[2,8000,128]{2,1,0:T(8,128)S(1)}, f32[10,2,8,128]{3,2,1,0:T(8,128)S(1)}, f32[10,2,8,128]{3,2,1,0:T(8,128)S(1)}, f32[8,128]{1,0:T(8,128)S(1)}) custom-call(bf16[256,2304]{1,0:T(8,128)(2,1)} %h_hbm.1, bf16[8000,2304]{1,0:T(8,128)(2,1)} %bitcast.9, f32[2,128]{1,0:T(2,128)} %bitcast.10, s32[2,128]{1,0:T(2,128)} %bitcast.11), custom_call_target="tpu_custom_call" | custom-call | tf_op jit(solution)/shard_map/stream/pallas_call | solution.py:233
  14.1 12.8 %exchange.1 = (f32[2,2,8,128]{3,2,1,0:T(8,128)S(1)}, f32[2,128]{1,0:T(2,128)S(1)}) custom-call(f32[8,128]{1,0:T(8,128)S(1)} %get-tuple-element.13.mix_ref), custom_call_target="tpu_custom_call" | custom-call | tf_op jit(solution)/shard_map/exchange/pallas_call | solution.py:255
  26.9 3.3 %finish.1 = (f32[1000,2,8,128]{3,2,1,0:T(8,128)}, f32[2,128]{1,0:T(2,128)}) custom-call(f32[2,8000,128]{2,1,0:T(8,128)S(1)} %get-tuple-element.10.c_ref, f32[10,2,8,128]{3,2,1,0:T(8,128)S(1)} %get-tuple-element.11.scale_ref, f32[10,2,8,128]{3,2,1,0:T(8,128)S(1)} %get-tuple-element.12.start_ref, f32[2,2,8,128]{3,2,1,0:T(8,128)S(1)} %get-tuple-element.14.ends_ref, ...), custom_call_target="tpu_custom_call" | custom-call | tf_op jit(solution)/shard_map/finish/pallas_call | solution.py:264

commit v5 on v4

v5 whole, which is shorter than its diff:
```python
import functools

import jax
import jax.numpy as jnp
from jax import lax
from jax.experimental import pallas as pl
from jax.experimental.pallas import tpu as pltpu
from jax.sharding import PartitionSpec as P

VOCAB_AXES = ('vocab', 'inner')
MESH = pl.DeviceIdType.MESH
LANES = 128
SUB = 8
BODY = 800
WIDE = 256
BLOCKS = 25


def hint(x, k):
    return x if isinstance(x, int) else pl.multiple_of(x, k)


def above(x, sub):
    total = x
    for d in (1, 2, 4):
        total = total + jnp.where(sub >= d, pltpu.roll(total, d, 0), 0.0)
    return total - x, jnp.broadcast_to(total[SUB - 1:SUB, :], (SUB, LANES))


def weigh(start, tops, tgt_v, zbuf, ebuf, c_ref, first):
    halves = len(tops)
    run = BODY // SUB
    sub = lax.broadcasted_iota(jnp.int32, (SUB, LANES), 0)
    out = []
    for i in range(halves):
        top = jnp.broadcast_to(jnp.max(tops[i], axis=0, keepdims=True), (SUB, LANES))
        sums = [jnp.zeros((SUB, LANES), jnp.float32)] * 4
        for j in range(run):
            e = jnp.exp(zbuf[i, pl.ds(j, SUB, stride=run), :] - top)
            ebuf[i, pl.ds(j * SUB, SUB), :] = e
            sums[j % 4] = sums[j % 4] + e
        running, total = above((sums[0] + sums[1]) + (sums[2] + sums[3]), sub)
        goal = tgt_v[pl.ds(i, 1), :] - start
        upto = jnp.where((goal >= BODY) & (sub == 0), total, 0.0)
        goal = goal - sub * run
        for j in range(run):
            running = running + ebuf[i, pl.ds(j * SUB, SUB), :]
            c_ref[i, pl.ds(first + j, SUB, stride=run), :] = running
            upto = jnp.where(goal == j, running, upto)
        out.append((top, total, upto))
    return out


def stream_kernel(h_hbm, w_hbm, inv_hbm, tgt_hbm,
                  c_ref, zbuf, top_ref, m_tile, s_tile, t_tile, tgt_v,
                  h_v, wbuf, inv_v, ebuf, in_sem, w_sem):
    rows, depth = h_v.shape
    width = w_hbm.shape[0]
    halves = rows // LANES
    count = width // BODY
    part = BODY // 2
    run = BODY // SUB
    me = lax.axis_index('vocab') * lax.axis_size('inner') + lax.axis_index('inner')
    sub = lax.broadcasted_iota(jnp.int32, (SUB, LANES), 0)

    def w_copy(t):
        here = pl.ds(hint(t * BODY, 16), BODY)
        return pltpu.make_async_copy(w_hbm.at[here, :], wbuf.at[here, :], w_sem.at[t])

    small = [pltpu.make_async_copy(h_hbm, h_v, in_sem.at[0]),
             pltpu.make_async_copy(inv_hbm, inv_v, in_sem.at[1]),
             pltpu.make_async_copy(tgt_hbm, tgt_v, in_sem.at[2])]
    for copy in small:
        copy.start()

    @pl.loop(0, count)
    def _(t):
        w_copy(t).start()

    for copy in small:
        copy.wait()

    def multiply(*accs):
        accs = (accs[:2], accs[2:])

        def push(k):
            for q in range(2):
                pltpu.matmul_push_rhs(h_v[:, pl.ds(k * WIDE, WIDE)], 0, q, transpose=True)

        def drain(t, slot):
            tops = [None] * halves
            for q in range(2):
                z = pltpu.matmul_pop(accs[q][slot])
                for i in range(halves):
                    zi = z[:, i * LANES:(i + 1) * LANES] * inv_v[pl.ds(i, 1), :]
                    zbuf[i, pl.ds(q * part, part), :] = zi
                    top = jnp.max(zi.reshape(part // SUB, SUB, LANES), axis=0)
                    tops[i] = top if q == 0 else jnp.maximum(tops[i], top)
            return tops

        def step(t, slot, first=False, final=False):
            w_copy(t).wait()
            for k in range(depth // WIDE):
                for q in range(2):
                    pltpu.matmul_acc_lhs(
                        accs[q][slot], wbuf[pl.ds(hint(t * BODY + q * part, 16), part), pl.ds(k * WIDE, WIDE)],
                        load_staged_rhs=0)
                if k < depth // WIDE - 1:
                    push(k + 1)
                elif not final:
                    push(0)
                if k == 1 and not first:
                    tops = drain(t - 1, 1 - slot)
                    start = (t - 1) * BODY
                    for i, (m, s, u) in enumerate(weigh(me * width + start, tops, tgt_v, zbuf, ebuf, c_ref, start)):
                        m_tile[t - 1, i] = m
                        s_tile[t - 1, i] = s
                        t_tile[t - 1, i] = u

        for q in range(2):
            for slot in range(2):
                pltpu.matmul_pop(accs[q][slot])
        push(0)
        step(0, 0, first=True)
        step(1, 1)

        @pl.loop(1, count // 2 - 1)
        def _(p):
            step(2 * p, 0)
            step(2 * p + 1, 1)

        step(count - 2, 0)
        step(count - 1, 1, final=True)
        for i, top in enumerate(drain(count - 1, 1)):
            top_ref[i] = top

    pl.run_scoped(multiply, *[pltpu.ACC(q)((part, rows), jnp.float32) for q in (0, 0, 1, 1)])


def exchange_kernel(n_vocab, n_inner, zbuf, top_ref, m_tile, s_tile, t_tile, tgt_v,
                    c_last, scale_ref, start_ref, ends_ref, ct_ref, ebuf, stats, send_sem, recv_sem):
    peers = n_vocab * n_inner
    halves = ct_ref.shape[0]
    my_vocab, my_inner = lax.axis_index('vocab'), lax.axis_index('inner')
    me = my_vocab * n_inner + my_inner

    far = sorted(((dv, di) for dv in range(n_vocab) for di in range(n_inner) if dv or di),
                 key=lambda o: -(min(o[0], n_vocab - o[0]) / 2 + min(o[1], n_inner - o[1])))

    def peer(dv, di):
        return {'vocab': lax.rem(my_vocab + dv, n_vocab), 'inner': lax.rem(my_inner + di, n_inner)}

    barrier = pltpu.get_barrier_semaphore()
    for offset in far:
        pl.semaphore_signal(barrier, inc=1, device_id=peer(*offset), device_id_type=MESH)

    count = m_tile.shape[0] + 1
    last = (count - 1) * BODY
    final = weigh(me * (count * BODY) + last, [top_ref[i] for i in range(halves)], tgt_v, zbuf, ebuf, c_last, 0)
    sub = lax.broadcasted_iota(jnp.int32, (SUB, LANES), 0)
    mix = jnp.zeros((SUB, LANES), jnp.float32)
    for i in range(halves):
        known = [(m_tile[t, i], s_tile[t, i], t_tile[t, i]) for t in range(count - 1)] + [final[i]]
        m = functools.reduce(jnp.maximum, [k[0] for k in known])
        s = jnp.zeros((SUB, LANES), jnp.float32)
        u = jnp.zeros((SUB, LANES), jnp.float32)
        for t in range(count):
            f = jnp.exp(known[t][0] - m)
            scale_ref[t, i] = f
            start_ref[t, i] = s
            s = s + known[t][1] * f
            u = u + known[t][2] * f
        mix = jnp.where((sub == 4 * i) | (sub == 4 * i + 1), m, mix)
        mix = jnp.where(sub == 4 * i + 2, s, mix)
        mix = jnp.where(sub == 4 * i + 3, jnp.sum(u, axis=0, keepdims=True), mix)
    stats[me] = mix
    pl.semaphore_wait(barrier, peers - 1)
    for offset in far:
        pltpu.make_async_remote_copy(
            src_ref=stats.at[me], dst_ref=stats.at[me], send_sem=send_sem, recv_sem=recv_sem,
            device_id=peer(*offset), device_id_type=MESH).start()

    everyone = stats.at[pl.ds(0, peers - 1)]
    done = pltpu.make_async_remote_copy(
        src_ref=everyone, dst_ref=everyone, send_sem=send_sem, recv_sem=recv_sem,
        device_id=peer(0, 0), device_id_type=MESH)
    done.wait_recv()

    peak = stats[0]
    for p in range(1, peers):
        peak = jnp.maximum(peak, stats[p])
    whole = jnp.zeros((SUB, LANES), jnp.float32)
    before = jnp.zeros((SUB, LANES), jnp.float32)
    for p in range(peers):
        mass = pltpu.roll(jnp.exp(stats[p] - peak), 2, 0) * stats[p]
        whole = whole + mass
        before = before + jnp.where(p < me, mass, 0.0)
    factor = pltpu.roll(jnp.exp(stats[me] - peak), 2, 0) / whole
    offset = before / whole
    reached = whole / pltpu.roll(whole, 1, 0)
    for i in range(halves):
        ct_ref[pl.ds(i, 1), :] = reached[4 * i + 3:4 * i + 4, :]
        ends_ref[0, i] = jnp.broadcast_to(factor[4 * i + 2:4 * i + 3, :], (SUB, LANES))
        ends_ref[1, i] = jnp.broadcast_to(offset[4 * i + 2:4 * i + 3, :], (SUB, LANES))
    done.wait_send()


def finish_kernel(c_ref, c_last, scale_ref, start_ref, ends_ref, ct_ref, out_hbm, ct_out, stage, sem):
    halves = c_ref.shape[0]
    parts = BODY // SUB // BLOCKS
    early = c_ref.shape[1] // SUB // BLOCKS
    target = pltpu.make_async_copy(ct_ref, ct_out, sem.at[1])
    target.start()

    def emit(b, source, origin):
        t = b // parts
        scale = [scale_ref[t, i] * ends_ref[0, i] for i in range(halves)]
        offset = [start_ref[t, i] * ends_ref[0, i] + ends_ref[1, i] for i in range(halves)]
        first = b * BLOCKS
        for k in range(BLOCKS):
            for i in range(halves):
                v = source[i, pl.ds(hint((first - origin + k) * SUB, SUB), SUB), :]
                stage[first + k, i] = v * scale[i] + offset[i]
        here = pl.ds(first, BLOCKS)
        pltpu.make_async_copy(stage.at[here], out_hbm.at[here], sem.at[0]).start()

    @pl.loop(0, early)
    def _(b):
        emit(b, c_ref, 0)

    @pl.loop(early, early + parts)
    def _(b):
        emit(b, c_last, early * BLOCKS)

    pltpu.make_async_copy(stage, out_hbm, sem.at[0]).wait()
    target.wait()


def solution(mesh):
    n_vocab, n_inner = mesh.shape['vocab'], mesh.shape['inner']
    peers = n_vocab * n_inner
    f32, bf16 = jnp.float32, jnp.bfloat16
    hbm = pl.BlockSpec(memory_space=pl.ANY)
    vmem = pl.BlockSpec(memory_space=pltpu.VMEM)

    def local_step(hidden, w_shard, inv_temp, target_id):
        rows, depth = hidden.shape
        width = w_shard.shape[1]
        halves = rows // LANES
        tiles = width // BODY
        small, early = (tiles, halves, SUB, LANES), (tiles - 1, halves, SUB, LANES)
        block = (halves, BODY, LANES)
        packed = (width // SUB, halves, SUB, LANES)
        c, *state = pl.pallas_call(
            stream_kernel,
            name='stream',
            out_shape=[pltpu.VMEM((halves, width - BODY, LANES), f32), pltpu.VMEM(block, f32),
                       pltpu.VMEM((halves, SUB, LANES), f32), pltpu.VMEM(early, f32), pltpu.VMEM(early, f32),
                       pltpu.VMEM(early, f32), pltpu.VMEM((halves, LANES), jnp.int32)],
            in_specs=[hbm] * 4,
            out_specs=[vmem] * 7,
            scratch_shapes=[
                pltpu.VMEM((rows, depth), bf16),
                pltpu.VMEM((width, depth), bf16),
                pltpu.VMEM((halves, LANES), f32),
                pltpu.VMEM(block, f32),
                pltpu.SemaphoreType.DMA((3,)),
                pltpu.SemaphoreType.DMA((tiles,)),
            ],
            compiler_params=pltpu.CompilerParams(vmem_limit_bytes=50 * 2**20),
        )(hidden, w_shard.T, inv_temp.reshape(halves, LANES), target_id.reshape(halves, LANES))
        shared = pl.pallas_call(
            functools.partial(exchange_kernel, n_vocab, n_inner),
            name='exchange',
            out_shape=[pltpu.VMEM(block, f32), pltpu.VMEM(small, f32), pltpu.VMEM(small, f32),
                       pltpu.VMEM((2, halves, SUB, LANES), f32), pltpu.VMEM((halves, LANES), f32)],
            in_specs=[vmem] * 6,
            out_specs=[vmem] * 5,
            scratch_shapes=[pltpu.VMEM(block, f32), pltpu.VMEM((peers, SUB, LANES), f32),
                            pltpu.SemaphoreType.DMA, pltpu.SemaphoreType.DMA],
            compiler_params=pltpu.CompilerParams(collective_id=0, has_side_effects=True, vmem_limit_bytes=4 * 2**20),
        )(*state)
        table, target = pl.pallas_call(
            finish_kernel,
            name='finish',
            out_shape=[pltpu.HBM(packed, f32), pltpu.HBM((halves, LANES), f32)],
            in_specs=[vmem] * 6,
            out_specs=[pl.BlockSpec(memory_space=pltpu.HBM)] * 2,
            scratch_shapes=[pltpu.VMEM(packed, f32), pltpu.SemaphoreType.DMA((2,))],
            compiler_params=pltpu.CompilerParams(vmem_limit_bytes=20 * 2**20),
        )(c, *shared)
        return table.transpose(0, 2, 1, 3).reshape(width, rows).T, target.reshape(rows)

    return jax.shard_map(local_step, mesh=mesh, in_specs=(P('dp', None), P(None, VOCAB_AXES), P('dp'), P('dp')), out_specs=(P('dp', VOCAB_AXES), P('dp')), check_vma=False)
```

time: 30.2 us -> 29.9 us (0.990)
  no operation moved by 1% of the time
where the time goes in v5:
time: 29.9 us; the launch traced here: 29.8 us
  Pallas kernels  29.2 us (98%)
  between operations  0.65 us (2%)
    pallas_call x1, Pallas kernels, local_step(): pl.pallas_call(stream_kernel, name='stream', out_shape=[pltpu.VMEM((halve...  13.2 us
    pallas_call x1, Pallas kernels, local_step(): pl.pallas_call(functools.partial(exchange_kernel, n_vocab, n_inner), name...  12.8 us
    pallas_call x1, Pallas kernels, local_step(): pl.pallas_call(finish_kernel, name='finish', out_shape=[pltpu.HBM(packed,...  3.25 us

profile of v5, /device:TPU:97, one launch (start us, length us, event | category | flops | bytes accessed | tf_op | source)
XLA Modules:
  0.0 29.8 jit_solution(8597506200435892427)
XLA Ops:
  0.6 13.2 %stream.1 = (f32[2,7200,128]{2,1,0:T(8,128)S(1)}, f32[2,800,128]{2,1,0:T(8,128)S(1)}, f32[2,8,128]{2,1,0:T(8,128)S(1)}, f32[9,2,8,128]{3,2,1,0:T(8,128)S(1)}, f3...) custom-call(bf16[256,2304]{1,0:T(8,128)(2,1)} %h_hbm.1, ...), custom_call_target="tpu_custom_call" | custom-call | tf_op jit(solution)/shard_map/stream/pallas_call | solution.py:254
  13.8 12.8 %exchange.1 = (f32[2,800,128]{2,1,0:T(8,128)S(1)}, f32[10,2,8,128]{3,2,1,0:T(8,128)S(1)}, f32[10,2,8,128]{3,2,1,0:T(8,128)S(1)}, f32[2,2,8,128]{3,2,1,0:T(8,128)S(1)}, f32[2,128]{1,0:T(2,128)S(1)}) custom-call(f32[2,800,128]{2,1,0:T(8,128)S(1)} %get-tuple-element.17.zbuf, f32[2,8,128]{2,1,0:T(8,128)S(1)} %get-tuple-element.18.top_ref, ...), custom_call_target="tpu_custom_call" | custom-call | tf_op jit(solution)/shard_map/exchange/pallas_call | solution.py:272
  26.6 3.3 %finish.1 = (f32[1000,2,8,128]{3,2,1,0:T(8,128)}, f32[2,128]{1,0:T(2,128)}) custom-call(f32[2,7200,128]{2,1,0:T(8,128)S(1)} %get-tuple-element.16.c_ref, f32[2,800,128]{2,1,0:T(8,128)S(1)} %get-tuple-element.23.c_last, f32[10,2,8,128]{3,2,1,0:T(8,128)S(1)} %get-tuple-element.24.scale_ref, f32[10,2,8,128]{3,2,1,0:T(8,128)S(1)} %get-tuple-element.25.start_ref, ...), custom_call_target="tpu_custom_call" | custom-call | tf_op jit(solution)/shard_map/finish/pallas_call | solution.py:283

commit v6 on v5

--- a/solution.py
+++ b/solution.py
@@ -14,6 +14,7 @@
 BODY = 800
 WIDE = 256
 BLOCKS = 25
+EARLY_K = 5
 
 
 def hint(x, k):
@@ -63,9 +64,11 @@
     me = lax.axis_index('vocab') * lax.axis_size('inner') + lax.axis_index('inner')
     sub = lax.broadcasted_iota(jnp.int32, (SUB, LANES), 0)
 
-    def w_copy(t):
+    def w_copy(t, piece):
         here = pl.ds(hint(t * BODY, 16), BODY)
-        return pltpu.make_async_copy(w_hbm.at[here, :], wbuf.at[here, :], w_sem.at[t])
+        cut = EARLY_K * WIDE
+        there = pl.ds(0, cut) if piece == 0 else pl.ds(cut, depth - cut)
+        return pltpu.make_async_copy(w_hbm.at[here, there], wbuf.at[here, there], w_sem.at[t, piece])
 
     small = [pltpu.make_async_copy(h_hbm, h_v, in_sem.at[0]),
              pltpu.make_async_copy(inv_hbm, inv_v, in_sem.at[1]),
@@ -75,7 +78,8 @@
 
     @pl.loop(0, count)
     def _(t):
-        w_copy(t).start()
+        w_copy(t, 0).start()
+        w_copy(t, 1).start()
 
     for copy in small:
         copy.wait()
@@ -99,8 +103,9 @@
             return tops
 
         def step(t, slot, first=False, final=False):
-            w_copy(t).wait()
             for k in range(depth // WIDE):
+                if k in (0, EARLY_K):
+                    w_copy(t, k // EARLY_K).wait()
                 for q in range(2):
                     pltpu.matmul_acc_lhs(
                         accs[q][slot], wbuf[pl.ds(hint(t * BODY + q * part, 16), part), pl.ds(k * WIDE, WIDE)],
@@ -111,6 +116,7 @@
                     push(0)
                 if k == 1 and not first:
                     tops = drain(t - 1, 1 - slot)
+                if k == EARLY_K and not first:
                     start = (t - 1) * BODY
                     for i, (m, s, u) in enumerate(weigh(me * width + start, tops, tgt_v, zbuf, ebuf, c_ref, start)):
                         m_tile[t - 1, i] = m
@@ -265,7 +271,7 @@
                 pltpu.VMEM((halves, LANES), f32),
                 pltpu.VMEM(block, f32),
                 pltpu.SemaphoreType.DMA((3,)),
-                pltpu.SemaphoreType.DMA((tiles,)),
+                pltpu.SemaphoreType.DMA((tiles, 2)),
             ],
             compiler_params=pltpu.CompilerParams(vmem_limit_bytes=50 * 2**20),
         )(hidden, w_shard.T, inv_temp.reshape(halves, LANES), target_id.reshape(halves, LANES))

time: 29.9 us -> 29.7 us (level)
  Pallas kernels: 29.2 us -> 28.9 us
where the time goes in v6:
time: 29.7 us; the launch traced here: 29.6 us
  Pallas kernels  28.9 us (97%)
  between operations  0.65 us (2%)
    pallas_call x1, Pallas kernels, local_step(): pl.pallas_call(stream_kernel, name='stream', out_shape=[pltpu.VMEM((halve...  12.9 us
    pallas_call x1, Pallas kernels, local_step(): pl.pallas_call(functools.partial(exchange_kernel, n_vocab, n_inner), name...  12.8 us
    pallas_call x1, Pallas kernels, local_step(): pl.pallas_call(finish_kernel, name='finish', out_shape=[pltpu.HBM(packed,...  3.25 us

profile of v6, /device:TPU:97, one launch (start us, length us, event | category | flops | bytes accessed | tf_op | source)
XLA Modules:
  0.0 29.6 jit_solution(6164340144647964037)
XLA Ops:
  0.6 12.9 %stream.1 = (f32[2,7200,128]{2,1,0:T(8,128)S(1)}, f32[2,800,128]{2,1,0:T(8,128)S(1)}, f32[2,8,128]{2,1,0:T(8,128)S(1)}, f32[9,2,8,128]{3,2,1,0:T(8,128)S(1)}, f3...) custom-call(bf16[256,2304]{1,0:T(8,128)(2,1)} %h_hbm.1, ...), custom_call_target="tpu_custom_call" | custom-call | tf_op jit(solution)/shard_map/stream/pallas_call | solution.py:260
  13.6 12.8 %exchange.1 = (f32[2,800,128]{2,1,0:T(8,128)S(1)}, f32[10,2,8,128]{3,2,1,0:T(8,128)S(1)}, f32[10,2,8,128]{3,2,1,0:T(8,128)S(1)}, f32[2,2,8,128]{3,2,1,0:T(8,128)S(1)}, f32[2,128]{1,0:T(2,128)S(1)}) custom-call(f32[2,800,128]{2,1,0:T(8,128)S(1)} %get-tuple-element.17.zbuf, f32[2,8,128]{2,1,0:T(8,128)S(1)} %get-tuple-element.18.top_ref, ...), custom_call_target="tpu_custom_call" | custom-call | tf_op jit(solution)/shard_map/exchange/pallas_call | solution.py:278
  26.3 3.3 %finish.1 = (f32[1000,2,8,128]{3,2,1,0:T(8,128)}, f32[2,128]{1,0:T(2,128)}) custom-call(f32[2,7200,128]{2,1,0:T(8,128)S(1)} %get-tuple-element.16.c_ref, f32[2,800,128]{2,1,0:T(8,128)S(1)} %get-tuple-element.23.c_last, f32[10,2,8,128]{3,2,1,0:T(8,128)S(1)} %get-tuple-element.24.scale_ref, f32[10,2,8,128]{3,2,1,0:T(8,128)S(1)} %get-tuple-element.25.start_ref, ...), custom_call_target="tpu_custom_call" | custom-call | tf_op jit(solution)/shard_map/finish/pallas_call | solution.py:289
